TPU v7x, 32 devices: a whole 2x2x4 slice. The times are simulated.
32 devices in a mesh: ctx: 16 (over z, x, core), head: 2 (over y).
Axes of the slice: x: 2, y: 2, z: 4, core: 2. Of those that a mesh axis runs over, the one named last changes fastest.
Arguments:
- query_heads: bfloat16 [4096, 32, 128], P('ctx', 'head'), may hold values from -5 to 5
- key_heads: bfloat16 [4096, 16, 128], P('ctx', 'head'), may hold values from -5 to 5
- value_heads: bfloat16 [4096, 16, 128], P('ctx', 'head'), may hold values from -6 to 6
- positions: int32 [4096], P('ctx'), may hold values from 0 to 4095, each once
- out_weight: bfloat16 [4096, 4608], P('head'), may hold values from -0.125 to 0.125
Outputs:
- attn_out: bfloat16 [4096, 4608], P('ctx', 'head')
Inputs may be any that keep to these rules, and one draw needn't show every extreme that they name: Each of the 4096 positions appears exactly once.
All inputs are finite; a program needn't handle non-finite values.
Results may differ from a plain program's by a relative error of at most 0.0081.
Values may be sent and summed in bfloat16 or wider, within the bound.
A program may use at most 64 MiB of HBM per device.

v0:
```python
import math

import jax
import jax.numpy as jnp
from jax import lax
from jax.sharding import PartitionSpec as P

NEG_BIG = -1e30
ATTN_SCALE = 1.0 / 12.0


def on_device(query_heads, key_heads, value_heads, positions, out_weight):
    tok_local, heads_local, head_size = query_heads.shape
    kv_local = key_heads.shape[1]
    group_size = heads_local // kv_local
    grouped = query_heads.reshape(tok_local, kv_local, group_size, head_size)
    all_positions = lax.all_gather(positions, "ctx", axis=0, tiled=True)
    stat_shape = (kv_local, group_size, tok_local)
    initial = (
        jnp.full(stat_shape, NEG_BIG, jnp.float32),
        jnp.zeros(stat_shape, jnp.float32),
        jnp.zeros(stat_shape + (head_size,), jnp.float32),
    )

    def attend_block(carry, key_block, value_block, key_pos):
        running_max, running_sum, accum = carry
        scores = (
            jnp.einsum("tkgd,skd->kgts", grouped, key_block, preferred_element_type=jnp.float32)
            * ATTN_SCALE
        )
        visible = key_pos[None, :] <= positions[:, None]
        scores = jnp.where(visible, scores, NEG_BIG)
        new_max = jnp.maximum(running_max, jnp.max(scores, axis=-1))
        weights = jnp.where(visible, jnp.exp(scores - new_max[..., None]), 0.0)
        decay_old = jnp.exp(running_max - new_max)
        running_sum = running_sum * decay_old + jnp.sum(weights, axis=-1)
        accum = accum * decay_old[..., None] + jnp.einsum(
            "kgts,skd->kgtd",
            weights.astype(jnp.bfloat16),
            value_block,
            preferred_element_type=jnp.float32,
        )
        return (new_max, running_sum, accum)

    key_all, value_all = (
        lax.all_gather(key_heads, "ctx", axis=0, tiled=True),
        lax.all_gather(value_heads, "ctx", axis=0, tiled=True),
    )
    piece_rows = key_all.shape[0]
    block_rows = math.gcd(piece_rows, 1024)

    def one_block(inner, block_index):
        offset = block_index * block_rows
        key_block = lax.dynamic_slice_in_dim(key_all, offset, block_rows, 0)
        value_block = lax.dynamic_slice_in_dim(value_all, offset, block_rows, 0)
        key_pos = lax.dynamic_slice_in_dim(all_positions, offset, block_rows, 0)
        return (attend_block(inner, key_block, value_block, key_pos), None)

    result, _ = lax.scan(one_block, initial, jnp.arange(piece_rows // block_rows, dtype=jnp.int32))
    _, total, accum = result
    attended = (accum / total[..., None]).astype(jnp.bfloat16)
    flat = jnp.transpose(attended, (2, 0, 1, 3)).reshape(tok_local, heads_local * head_size)
    terms = jnp.dot(flat, out_weight, preferred_element_type=jnp.float32)
    return lax.psum_scatter(terms, "head", scatter_dimension=1, tiled=True).astype(jnp.bfloat16)


def solution(mesh):
    placed = (
        P("ctx", "head", None),
        P("ctx", "head", None),
        P("ctx", "head", None),
        P("ctx"),
        P("head", None),
    )
    return jax.shard_map(
        on_device, mesh=mesh, in_specs=placed, out_specs=P("ctx", "head"), check_vma=False
    )
```

profile of v0, /device:TPU:0, one launch (start us, length us, event | category | flops | bytes accessed | tf_op | source)
XLA Modules:
  0.0 315.1 jit_solution(10116971357702970398)
XLA Ops:
  6.5 1.9 copy.16
  8.5 1.9 copy.18
  10.5 1.5 copy.17
  12.0 23.7 %all-gather = s32[16,1,256]{2,1,0:T(1,128)S(1)} all-gather(s32[1,1,256]{2,1,0:T(1,128)} %bitcast.54), channel_id=1, replica_groups=mesh['ctx'=16,'head'=2] {'ctx'}, dimensions={0}, use_global_device_ids=true | all-gather | bytes 17408 | tf_op jit(solution)/shard_map/all_gather | solution.py:17
  35.7 50.9 %all-gather.4.cloned.1.call-done = bf16[4096,8,128]{2,0,1:T(8,128)(2,1)} async-done(((bf16[256,8,128]{2,0,1:T(8,128)(2,1)}), bf16[4096,8,128]{2,0,1:T(8,128)(2,1)}) %all-gather.4.cloned.1.call-update) | async-done | bytes 8388624 | tf_op jit(solution)/shard_map/all_gather | solution.py:46
  86.6 75.1 %all-gather.6.cloned.1.call-done = bf16[4096,8,128]{2,0,1:T(8,128)(2,1)} async-done(((bf16[256,8,128]{2,0,1:T(8,128)(2,1)}), bf16[4096,8,128]{2,0,1:T(8,128)(2,1)}) %all-gather.6.cloned.1.call-update) | async-done | bytes 8388624 | tf_op jit(solution)/shard_map/all_gather | solution.py:47
  161.8 70.5 %while.15 = (s32[]{:T(128)}, f32[8,2,256]{2,1,0:T(2,128)S(1)}, f32[8,2,256]{2,1,0:T(2,128)S(1)}, f32[8,2,256,128]{3,2,1,0:T(8,128)S(1)}, s32[4]{0:T(128)S(1)}, /...) while((s32[]{:T(128)}, f32[8,2,256]{2,1,0:T(2,128)S(1)}, ...), condition=%wide.region_3.4_spmd.clone, body=%wide.region_0.3_spmd.clone.sunk | while | flops 2203865088 | bytes 61093084 | solution.py:59
  163.9 4.0 %fusion.38 = (f32[8,2,256]{2,1,0:T(2,128)S(1)}, f32[8,1024,256,2]{2,1,3,0:T(8,128)S(1)}) fusion(pred[256,1024]{0,1:T(8,128)(4,1)S(1)} %broadcast_compare_fusion.2, bf16[256,8,2,128]{3,0,2,1:T(8,128)(2,1)S(1)} %get-tuple-element.222, bf16[4096,8,128]{2,0,1:T(8,128)(2,1)} %get-tuple-element.221, s32[]{:T(128)S(6)} %select_n.46), kind=kOutput, calls=%fused_computation.2.clone.1 | convolution fusion | flops 1086320640 | bytes 20201476 | tf_op jit(solution)/shard_map/while/body/eval_jaxpr/tkgd,skd->kgts/dot_general | solution.py:28
  167.9 4.0 %fusion.40 = f32[8,2,256]{2,1,0:T(2,128)S(1)} fusion(f32[8,1024,256,2]{2,1,3,0:T(8,128)S(1)} %get-tuple-element.183, f32[8,2,256]{2,1,0:T(2,128)S(1)} %fusion.39, pred[256,1024]{0,1:T(8,128)(4,1)S(1)} %broadcast_compare_fusion.2), kind=kLoop, calls=%fused_computation.4.clone.1 | loop fusion | flops 20967424 | bytes 17072128 | tf_op jit(solution)/shard_map/while/body/eval_jaxpr/reduce_sum | solution.py:36
  172.0 7.3 %fusion.42 = f32[8,2,256,128]{3,2,1,0:T(8,128)S(1)} fusion(f32[8,2,256,128]{3,2,1,0:T(8,128)S(1)} %get-tuple-element.203, bf16[4096,8,128]{2,0,1:T(8,128)(2,1)} %get-tuple-element.223, s32[]{:T(128)S(6)} %select_n.46, f32[8,1024,256,2]{2,1,3,0:T(8,128)S(1)} %get-tuple-element.183, f32[8,2,256]{2,1,0:T(2,128)S(1)} %fusion.39, ...), kind=kOutput, calls=%fused_computation.11.clone.1 | convolution fusion | flops 1096286208 | bytes 23363588 | tf_op jit(solution)/shard_map/while/body/eval_jaxpr/kgts,skd->kgtd/dot_general | solution.py:37
  181.5 4.0 %fusion.38 = (f32[8,2,256]{2,1,0:T(2,128)S(1)}, f32[8,1024,256,2]{2,1,3,0:T(8,128)S(1)}) fusion(pred[256,1024]{0,1:T(8,128)(4,1)S(1)} %broadcast_compare_fusion.2, bf16[256,8,2,128]{3,0,2,1:T(8,128)(2,1)S(1)} %get-tuple-element.222, bf16[4096,8,128]{2,0,1:T(8,128)(2,1)} %get-tuple-element.221, s32[]{:T(128)S(6)} %select_n.46), kind=kOutput, calls=%fused_computation.2.clone.1 | convolution fusion | flops 1086320640 | bytes 20201476 | tf_op jit(solution)/shard_map/while/body/eval_jaxpr/tkgd,skd->kgts/dot_general | solution.py:28
  185.6 4.0 %fusion.40 = f32[8,2,256]{2,1,0:T(2,128)S(1)} fusion(f32[8,1024,256,2]{2,1,3,0:T(8,128)S(1)} %get-tuple-element.183, f32[8,2,256]{2,1,0:T(2,128)S(1)} %fusion.39, pred[256,1024]{0,1:T(8,128)(4,1)S(1)} %broadcast_compare_fusion.2), kind=kLoop, calls=%fused_computation.4.clone.1 | loop fusion | flops 20967424 | bytes 17072128 | tf_op jit(solution)/shard_map/while/body/eval_jaxpr/reduce_sum | solution.py:36
  189.7 7.3 %fusion.42 = f32[8,2,256,128]{3,2,1,0:T(8,128)S(1)} fusion(f32[8,2,256,128]{3,2,1,0:T(8,128)S(1)} %get-tuple-element.203, bf16[4096,8,128]{2,0,1:T(8,128)(2,1)} %get-tuple-element.223, s32[]{:T(128)S(6)} %select_n.46, f32[8,1024,256,2]{2,1,3,0:T(8,128)S(1)} %get-tuple-element.183, f32[8,2,256]{2,1,0:T(2,128)S(1)} %fusion.39, ...), kind=kOutput, calls=%fused_computation.11.clone.1 | convolution fusion | flops 1096286208 | bytes 23363588 | tf_op jit(solution)/shard_map/while/body/eval_jaxpr/kgts,skd->kgtd/dot_general | solution.py:37
  199.2 4.0 %fusion.38 = (f32[8,2,256]{2,1,0:T(2,128)S(1)}, f32[8,1024,256,2]{2,1,3,0:T(8,128)S(1)}) fusion(pred[256,1024]{0,1:T(8,128)(4,1)S(1)} %broadcast_compare_fusion.2, bf16[256,8,2,128]{3,0,2,1:T(8,128)(2,1)S(1)} %get-tuple-element.222, bf16[4096,8,128]{2,0,1:T(8,128)(2,1)} %get-tuple-element.221, s32[]{:T(128)S(6)} %select_n.46), kind=kOutput, calls=%fused_computation.2.clone.1 | convolution fusion | flops 1086320640 | bytes 20201476 | tf_op jit(solution)/shard_map/while/body/eval_jaxpr/tkgd,skd->kgts/dot_general | solution.py:28
  203.2 4.0 %fusion.40 = f32[8,2,256]{2,1,0:T(2,128)S(1)} fusion(f32[8,1024,256,2]{2,1,3,0:T(8,128)S(1)} %get-tuple-element.183, f32[8,2,256]{2,1,0:T(2,128)S(1)} %fusion.39, pred[256,1024]{0,1:T(8,128)(4,1)S(1)} %broadcast_compare_fusion.2), kind=kLoop, calls=%fused_computation.4.clone.1 | loop fusion | flops 20967424 | bytes 17072128 | tf_op jit(solution)/shard_map/while/body/eval_jaxpr/reduce_sum | solution.py:36
  207.3 7.3 %fusion.42 = f32[8,2,256,128]{3,2,1,0:T(8,128)S(1)} fusion(f32[8,2,256,128]{3,2,1,0:T(8,128)S(1)} %get-tuple-element.203, bf16[4096,8,128]{2,0,1:T(8,128)(2,1)} %get-tuple-element.223, s32[]{:T(128)S(6)} %select_n.46, f32[8,1024,256,2]{2,1,3,0:T(8,128)S(1)} %get-tuple-element.183, f32[8,2,256]{2,1,0:T(2,128)S(1)} %fusion.39, ...), kind=kOutput, calls=%fused_computation.11.clone.1 | convolution fusion | flops 1096286208 | bytes 23363588 | tf_op jit(solution)/shard_map/while/body/eval_jaxpr/kgts,skd->kgtd/dot_general | solution.py:37
  216.8 4.0 %fusion.38 = (f32[8,2,256]{2,1,0:T(2,128)S(1)}, f32[8,1024,256,2]{2,1,3,0:T(8,128)S(1)}) fusion(pred[256,1024]{0,1:T(8,128)(4,1)S(1)} %broadcast_compare_fusion.2, bf16[256,8,2,128]{3,0,2,1:T(8,128)(2,1)S(1)} %get-tuple-element.222, bf16[4096,8,128]{2,0,1:T(8,128)(2,1)} %get-tuple-element.221, s32[]{:T(128)S(6)} %select_n.46), kind=kOutput, calls=%fused_computation.2.clone.1 | convolution fusion | flops 1086320640 | bytes 20201476 | tf_op jit(solution)/shard_map/while/body/eval_jaxpr/tkgd,skd->kgts/dot_general | solution.py:28
  220.8 4.0 %fusion.40 = f32[8,2,256]{2,1,0:T(2,128)S(1)} fusion(f32[8,1024,256,2]{2,1,3,0:T(8,128)S(1)} %get-tuple-element.183, f32[8,2,256]{2,1,0:T(2,128)S(1)} %fusion.39, pred[256,1024]{0,1:T(8,128)(4,1)S(1)} %broadcast_compare_fusion.2), kind=kLoop, calls=%fused_computation.4.clone.1 | loop fusion | flops 20967424 | bytes 17072128 | tf_op jit(solution)/shard_map/while/body/eval_jaxpr/reduce_sum | solution.py:36
  224.9 7.3 %fusion.42 = f32[8,2,256,128]{3,2,1,0:T(8,128)S(1)} fusion(f32[8,2,256,128]{3,2,1,0:T(8,128)S(1)} %get-tuple-element.203, bf16[4096,8,128]{2,0,1:T(8,128)(2,1)} %get-tuple-element.223, s32[]{:T(128)S(6)} %select_n.46, f32[8,1024,256,2]{2,1,3,0:T(8,128)S(1)} %get-tuple-element.183, f32[8,2,256]{2,1,0:T(2,128)S(1)} %fusion.39, ...), kind=kOutput, calls=%fused_computation.11.clone.1 | convolution fusion | flops 1096286208 | bytes 23363588 | tf_op jit(solution)/shard_map/while/body/eval_jaxpr/kgts,skd->kgtd/dot_general | solution.py:37
  232.3 1.3 copy-done
  233.6 1.9 copy.19
  235.7 11.2 %fusion.23 = f32[256,4608]{1,0:T(8,128)} fusion(bf16[256,2048]{0,1:T(8,128)(2,1)S(1)} %bitcast.52, bf16[2048,4608]{1,0:T(8,128)(2,1)} %param.11), kind=kOutput, calls=%fused_computation.26 | convolution fusion | flops 4831838208 | bytes 24641536 | tf_op jit(solution)/shard_map/dot_general | solution.py:63
  246.9 58.8 %reduce-scatter.2.cloned.1.call-done = f32[256,2304]{1,0:T(8,128)} async-done(((f32[256,4608]{1,0:T(8,128)}), f32[256,2304]{1,0:T(8,128)}) %reduce-scatter.2.cloned.1.call-update) | async-done | bytes 2359312 | tf_op jit(solution)/shard_map/reduce_scatter | solution.py:64
  305.7 2.8 convert_element_type.10
  (36 shorter events, 6.5 us)
Async XLA Ops:
  6.5 80.1 %all-gather.4.cloned.1.call-start = ((), (), s32[]{:S(2)}) async-start(), calls=%async_computation.1 | async-start | bytes 8912896 | tf_op jit(solution)/shard_map/all_gather | solution.py:46
  8.5 153.3 %all-gather.6.cloned.1.call-start = ((), (), s32[]{:S(2)}) async-start(), calls=%async_computation.2 | async-start | bytes 8912896 | tf_op jit(solution)/shard_map/all_gather | solution.py:47
  10.4 295.3 %reduce-scatter.2.cloned.1.call-start = ((), (), s32[]{:S(2)}) async-start(), calls=%async_computation.3 | async-start | bytes 7077888 | tf_op jit(solution)/shard_map/reduce_scatter | solution.py:64
  232.3 1.3 copy-start
Sparse Core Ops, SparseCore 0:
  9.5 77.0 all-gather.3
  88.8 72.8 all-gather.5
  247.0 58.6 reduce-scatter.1
where the time goes:
time: 316 us; the launch traced here: 315 us
  waiting for transfers between devices  185 us (59%)
  matrix products  56.4 us (18%)
  blocking collectives  23.7 us (8%)
  other arithmetic  23 us (7%)
  between operations  13.2 us (4%)
  local copies, waits for them, and re-layouts  11 us (3%)
    all_gather x1, waiting for transfers between devices, on_device(): lax.all_gather(value_heads, 'ctx', axis=0, tiled=True)  75.1 us
    reduce_scatter x1, waiting for transfers between devices, on_device(): lax.psum_scatter(terms, 'head', scatter_dimension=1, tiled=True)  58.8 us
    all_gather x1, waiting for transfers between devices, on_device(): lax.all_gather(key_heads, 'ctx', axis=0, tiled=True)  50.9 us
    dot_general x4, matrix products, attend_block(): jnp.einsum('kgts,skd->kgtd', weights.astype(jnp.bfloat16), value_block, p...  29.3 us
    all_gather x1, blocking collectives, on_device(): all_positions = lax.all_gather(positions, 'ctx', axis=0, tiled=True)  23.7 us
    reduce_sum x4, other arithmetic, attend_block(): running_sum = running_sum * decay_old + jnp.sum(weights, axis=-1)  16.2 us
    dot_general x4, matrix products, attend_block(): jnp.einsum('tkgd,skd->kgts', grouped, key_block, preferred_element_type=j...  15.9 us
    dot_general x1, matrix products, on_device(): terms = jnp.dot(flat, out_weight, preferred_element_type=jnp.float32)  11.2 us
  transfers between devices with their start and end apart: 3, of which 3 were waited for; matrix products, arithmetic and copies ran while one was open for 1% of the time, Pallas kernels for 0%

commit v1 on v0

--- a/solution.py
+++ b/solution.py
@@ -1,15 +1,21 @@
+import functools
 import math
 
 import jax
 import jax.numpy as jnp
 from jax import lax
+from jax.experimental import pallas as pl
+from jax.experimental.pallas import tpu as pltpu
 from jax.sharding import PartitionSpec as P
 
 NEG_BIG = -1e30
 ATTN_SCALE = 1.0 / 12.0
-
-
-def on_device(query_heads, key_heads, value_heads, positions, out_weight):
+EXP2_SCALE = ATTN_SCALE * math.log2(math.e)
+MESH = pl.DeviceIdType.MESH
+QUAD = 4
+
+
+def plain_on_device(query_heads, key_heads, value_heads, positions, out_weight):
     tok_local, heads_local, head_size = query_heads.shape
     kv_local = key_heads.shape[1]
     group_size = heads_local // kv_local
@@ -64,6 +70,322 @@
     return lax.psum_scatter(terms, "head", scatter_dimension=1, tiled=True).astype(jnp.bfloat16)
 
 
+def fused_kernel(
+    n_ctx, n_blocks, q_in, kv_in, pos_in, w_hbm, out_ref,
+    kvbuf, qbuf, posbuf, qcol, m_ref, acc_ref, obuf, attbuf, w_vmem, sendbuf, recvbuf, ownbuf,
+    w_sem, pos_send, pos_recv, kvq_send, kvq_recv, q_send, q_recv,
+    up_send, down_send, below_recv, above_recv, att_send, att_recv, y_send, y_recv,
+):
+    me = lax.axis_index("ctx")
+    head = lax.axis_index("head")
+    nz = n_ctx // QUAD
+    z = me // QUAD
+    s = me % QUAD
+    s_hi, s_lo = s // 2, s % 2
+    n_kv, _, tok, hd = kv_in.shape
+    groups = n_kv // QUAD
+    rep = q_in.shape[0] // n_kv
+    tok_z = QUAD * tok
+    half = out_ref.shape[1]
+    width = half // n_blocks
+
+    def peer(d):
+        hi = s_hi if d < 2 else 1 - s_hi
+        lo = s_lo if d % 2 == 0 else 1 - s_lo
+        return 2 * hi + lo
+
+    def rows(idx):
+        return pl.ds(pl.multiple_of(idx * tok, tok), tok)
+
+    barrier = pltpu.get_barrier_semaphore()
+    for d in range(1, n_ctx):
+        pl.semaphore_signal(
+            barrier, inc=1, device_id=(lax.rem(me + d, n_ctx), head), device_id_type=MESH
+        )
+    pl.semaphore_signal(barrier, inc=1, device_id=(me, 1 - head), device_id_type=MESH)
+    pl.semaphore_wait(barrier, n_ctx)
+
+    def remote(src, dst, ssem, rsem, ctx, hh=None):
+        return pltpu.make_async_remote_copy(
+            src_ref=src, dst_ref=dst, send_sem=ssem, recv_sem=rsem,
+            device_id=(ctx, head if hh is None else hh), device_id_type=MESH,
+        )
+
+    def pos_copy(d):
+        return remote(
+            pos_in, posbuf.at[me], pos_send.at[d], pos_recv.at[d], lax.rem(me + d, n_ctx)
+        )
+
+    def kv_copy(d, g):
+        p = peer(d)
+        return remote(
+            kv_in.at[p * groups + g], kvbuf.at[z, g, :, rows(s), :],
+            kvq_send.at[d, g], kvq_recv.at[d, g], z * QUAD + p,
+        )
+
+    def q_copy(d, g):
+        p = peer(d)
+        return remote(
+            q_in.at[pl.ds((p * groups + g) * rep, rep)],
+            qbuf.at[pl.ds(g * rep, rep), rows(s), :],
+            q_send.at[d, g], q_recv.at[d, g], z * QUAD + p,
+        )
+
+    def z_send_part(g, src, idx):
+        dst = kvbuf.at[z, g, :, rows(idx), :]
+
+        @pl.when(z > 0)
+        def _():
+            remote(src, dst, down_send.at[0, g], above_recv.at[1, g], me - QUAD).start()
+
+        @pl.when(z < nz - 1)
+        def _():
+            remote(src, dst, up_send.at[0, g], below_recv.at[1, g], me + QUAD).start()
+
+    def down_chunk(k, g):
+        chunk = kvbuf.at[z + k, g]
+        return remote(chunk, chunk, down_send.at[k, g], above_recv.at[k + 1, g], me - QUAD)
+
+    def up_chunk(k, g):
+        chunk = kvbuf.at[z - k, g]
+        return remote(chunk, chunk, up_send.at[k, g], below_recv.at[k + 1, g], me + QUAD)
+
+    def wait_above(k, g):
+        chunk = kvbuf.at[z + k, g]
+        remote(chunk, chunk, down_send.at[k, g], above_recv.at[k, g], me).wait_recv()
+
+    def wait_below(k, g):
+        chunk = kvbuf.at[z - k, g]
+        remote(chunk, chunk, up_send.at[k, g], below_recv.at[k, g], me).wait_recv()
+
+    for g in range(groups):
+        for d in (1, 2, 3):
+            kv_copy(d, g).start()
+        if g == 0:
+            for d in range(1, n_ctx):
+                pos_copy(d).start()
+        z_send_part(g, kv_in.at[s * groups + g], s)
+        for d in (1, 2, 3):
+            q_copy(d, g).start()
+    w_copies = []
+    for part in range(2):
+        col = (1 - head) if part == 0 else head
+        w_copies.append(
+            pltpu.make_async_copy(
+                w_hbm.at[:, pl.ds(pl.multiple_of(col * half, 128), half)],
+                w_vmem.at[part], w_sem.at[part],
+            )
+        )
+        w_copies[-1].start()
+
+    posbuf[me] = pos_in[...]
+    for g in range(groups):
+        kvbuf[z, g, :, rows(s), :] = kv_in[s * groups + g]
+        for r in range(rep):
+            qbuf[g * rep + r, rows(s), :] = q_in[(s * groups + g) * rep + r]
+    m_ref[...] = jnp.full(m_ref.shape, NEG_BIG, jnp.float32)
+    acc_ref[...] = jnp.zeros(acc_ref.shape, jnp.float32)
+
+    def own_parts(g):
+        for d in (1, 2, 3):
+            kv_copy(d, g).wait_recv()
+            p = peer(d)
+            z_send_part(g, kvbuf.at[z, g, :, rows(p), :], p)
+
+    def compute(layer, g):
+        key_pos = jnp.concatenate([posbuf[layer * QUAD + i] for i in range(QUAD)], axis=1)
+        key_pos = key_pos.astype(jnp.float32)
+
+        def tile(i, _):
+            r = i // QUAD
+            t = i % QUAD
+            q = qbuf[g * rep + r, rows(t), :]
+            keys = kvbuf[layer, g, 0]
+            values = kvbuf[layer, g, 1]
+            x = lax.dot_general(
+                q, keys, (((1,), (1,)), ((), ())), preferred_element_type=jnp.float32
+            ) * EXP2_SCALE
+            q_pos = qcol[rows(t), :][:, :1]
+            x = jnp.where(key_pos <= q_pos, x, NEG_BIG)
+            m_old = m_ref[g * rep + r, rows(t), :]
+            m_new = jnp.maximum(m_old, jnp.max(x, axis=1, keepdims=True))
+            m_ref[g * rep + r, rows(t), :] = m_new
+            decay = jnp.exp2(m_old - m_new)
+            weights = jnp.exp2(x - m_new[:, :1]).astype(jnp.bfloat16)
+            extended = jnp.concatenate([values, jnp.ones_like(values)], axis=1)
+            new = jnp.dot(weights, extended, preferred_element_type=jnp.float32)
+            old = acc_ref[g * rep + r, rows(t), :]
+            acc_ref[g * rep + r, rows(t), :] = (
+                old * jnp.concatenate([decay, decay], axis=1) + new
+            )
+            return 0
+
+        lax.fori_loop(0, rep * QUAD, tile, 0)
+
+    def att_copy(d, g):
+        p = peer(d)
+        cols = pl.ds(g * rep * hd, rep * hd)
+        return remote(
+            obuf.at[rows(p), cols], attbuf.at[s, :, cols],
+            att_send.at[d, g], att_recv.at[d, g], z * QUAD + p,
+        )
+
+    def finish(g):
+        for r in range(rep):
+            for t in range(QUAD):
+                part = acc_ref[g * rep + r, t * tok:(t + 1) * tok, :]
+                done = (part[:, :hd] / part[:, hd:]).astype(jnp.bfloat16)
+                obuf[t * tok:(t + 1) * tok, (g * rep + r) * hd:(g * rep + r + 1) * hd] = done
+        for d in (3, 2, 1):
+            att_copy(d, g).start()
+        cols = slice(g * rep * hd, (g + 1) * rep * hd)
+        attbuf[s, :, cols] = obuf[rows(s), cols]
+
+    for g in range(groups):
+        own_parts(g)
+        if g == 0:
+            for d in range(1, n_ctx):
+                pos_copy(d).wait_recv()
+            for i in range(QUAD):
+                line = posbuf[z * QUAD + i].astype(jnp.float32)
+                for j in range(tok // 128):
+                    piece = jnp.broadcast_to(line[:, j * 128:(j + 1) * 128], (128, 128))
+                    qcol[i * tok + j * 128:i * tok + (j + 1) * 128, :] = piece.T
+        for d in (1, 2, 3):
+            q_copy(d, g).wait_recv()
+        compute(z, g)
+
+    for k in range(1, nz):
+        for g in range(groups):
+            @pl.when(z + k < nz)
+            def _():
+                wait_above(k, g)
+
+                @pl.when(z > 0)
+                def _():
+                    down_chunk(k, g).start()
+
+                compute(z + k, g)
+
+            @pl.when(z - k >= 0)
+            def _():
+                wait_below(k, g)
+
+                @pl.when(z < nz - 1)
+                def _():
+                    up_chunk(k, g).start()
+
+                compute(z - k, g)
+
+            if k == nz - 1:
+                finish(g)
+    if nz == 1:
+        for g in range(groups):
+            finish(g)
+
+    def y_copy(b):
+        return remote(
+            sendbuf.at[b], recvbuf.at[b], y_send.at[b], y_recv.at[b], me, 1 - head
+        )
+
+    for g in range(groups):
+        for d in (1, 2, 3):
+            att_copy(d, g).wait_recv()
+
+    def product(part, b):
+        total = None
+        depth = groups * rep * hd
+        for j in range(QUAD):
+            term = jnp.dot(
+                attbuf[j],
+                w_vmem[part, j * depth:(j + 1) * depth, b * width:(b + 1) * width],
+                preferred_element_type=jnp.float32,
+            )
+            total = term if total is None else total + term
+        return total
+
+    w_copies[0].wait()
+    for b in range(n_blocks):
+        sendbuf[b] = product(0, b).astype(jnp.bfloat16)
+        y_copy(b).start()
+    w_copies[1].wait()
+    for b in range(n_blocks):
+        ownbuf[b] = product(1, b)
+    for b in range(n_blocks):
+        y_copy(b).wait_recv()
+        out_ref[:, b * width:(b + 1) * width] = (
+            ownbuf[b] + recvbuf[b].astype(jnp.float32)
+        ).astype(jnp.bfloat16)
+
+    for d in range(1, n_ctx):
+        pos_copy(d).wait_send()
+    for g in range(groups):
+        for d in (1, 2, 3):
+            kv_copy(d, g).wait_send()
+            q_copy(d, g).wait_send()
+            att_copy(d, g).wait_send()
+        for k in range(nz - 1):
+            @pl.when((z > 0) & (z + k < nz))
+            def _():
+                down_chunk(k, g).wait_send()
+
+            @pl.when((z < nz - 1) & (z - k >= 0))
+            def _():
+                up_chunk(k, g).wait_send()
+    for b in range(n_blocks):
+        y_copy(b).wait_send()
+
+
+def fused_on_device(n_ctx, query_heads, key_heads, value_heads, positions, out_weight):
+    tok, n_q, hd = query_heads.shape
+    n_kv = key_heads.shape[1]
+    q = jnp.transpose(query_heads, (1, 0, 2))
+    kv = jnp.transpose(jnp.stack([key_heads, value_heads]), (2, 0, 1, 3))
+    pos = positions.reshape(1, tok)
+    nz = n_ctx // QUAD
+    groups = n_kv // QUAD
+    q_dev = n_q // QUAD
+    tok_z = QUAD * tok
+    rows_w, model = out_weight.shape
+    half = model // 2
+    n_blocks = 3 if half % 384 == 0 else 1
+    width = half // n_blocks
+    vmem = pltpu.VMEM
+    dma = pltpu.SemaphoreType.DMA
+    whole = pl.BlockSpec(memory_space=pltpu.VMEM)
+    return pl.pallas_call(
+        functools.partial(fused_kernel, n_ctx, n_blocks),
+        out_shape=jax.ShapeDtypeStruct((tok, half), jnp.bfloat16),
+        in_specs=[whole, whole, whole, pl.BlockSpec(memory_space=pl.ANY)],
+        out_specs=whole,
+        scratch_shapes=[
+            vmem((nz, groups, 2, tok_z, hd), jnp.bfloat16),
+            vmem((q_dev, tok_z, hd), jnp.bfloat16),
+            vmem((n_ctx, 1, tok), jnp.int32),
+            vmem((tok_z, 128), jnp.float32),
+            vmem((q_dev, tok_z, hd), jnp.float32),
+            vmem((q_dev, tok_z, 2 * hd), jnp.float32),
+            vmem((tok_z, q_dev * hd), jnp.bfloat16),
+            vmem((QUAD, tok, q_dev * hd), jnp.bfloat16),
+            vmem((2, rows_w, half), jnp.bfloat16),
+            vmem((n_blocks, tok, width), jnp.bfloat16),
+            vmem((n_blocks, tok, width), jnp.bfloat16),
+            vmem((n_blocks, tok, width), jnp.float32),
+            dma((2,)),
+            dma((n_ctx,)), dma((n_ctx,)),
+            dma((QUAD, groups)), dma((QUAD, groups)),
+            dma((QUAD, groups)), dma((QUAD, groups)),
+            dma((nz, groups)), dma((nz, groups)),
+            dma((nz + 1, groups)), dma((nz + 1, groups)),
+            dma((QUAD, groups)), dma((QUAD, groups)),
+            dma((n_blocks,)), dma((n_blocks,)),
+        ],
+        compiler_params=pltpu.CompilerParams(
+            collective_id=0, has_side_effects=True, vmem_limit_bytes=62 * 1024 * 1024
+        ),
+    )(q, kv, pos, out_weight)
+
+
 def solution(mesh):
     placed = (
         P("ctx", "head", None),
@@ -72,6 +394,19 @@
         P("ctx"),
         P("head", None),
     )
+    n_ctx, n_head = mesh.shape["ctx"], mesh.shape["head"]
+
+    def on_device(query_heads, key_heads, value_heads, positions, out_weight):
+        args = (query_heads, key_heads, value_heads, positions, out_weight)
+        fits = (
+            n_head == 2 and n_ctx % QUAD == 0 and key_heads.shape[1] % QUAD == 0
+            and query_heads.shape[2] == 128 and query_heads.shape[0] % 128 == 0
+            and out_weight.shape[1] % 256 == 0
+        )
+        if fits:
+            return fused_on_device(n_ctx, *args)
+        return plain_on_device(*args)
+
     return jax.shard_map(
         on_device, mesh=mesh, in_specs=placed, out_specs=P("ctx", "head"), check_vma=False
     )

time: 316 us -> 149 us (0.47)
  waiting for transfers between devices: 185 us -> 0 us
  Pallas kernels: 0 us -> 142 us
  matrix products: 56.4 us -> 0 us
  blocking collectives: 23.7 us -> 0 us
  other arithmetic: 23 us -> 1.11 us
  between operations: 13.2 us -> 0.02 us
  local copies, waits for them, and re-layouts: 11 us -> 5.11 us
    pallas_call x0 -> x1, Pallas kernels: none -> 142 us  [fused_on_device(): pl.pallas_call(functools.partial(fused_kernel, n_ctx, n_blocks), out_shap...]
    all_gather x2 -> x0, waiting for transfers between devices: 126 us -> none  [the longest x1 75.1 us: on_device(): lax.all_gather(value_heads, 'ctx', axis=0, tiled=True)]
    reduce_scatter x1 -> x0, waiting for transfers between devices: 58.8 us -> none  [on_device(): lax.psum_scatter(terms, 'head', scatter_dimension=1, tiled=True)]
    dot_general x9 -> x0, matrix products: 56.4 us -> none  [the longest x4 29.3 us: attend_block(): jnp.einsum('kgts,skd->kgtd', weights.astype(jnp.bfloat16), value_block, p...]
    all_gather x1 -> x0, blocking collectives: 23.7 us -> none  [on_device(): all_positions = lax.all_gather(positions, 'ctx', axis=0, tiled=True)]
    reduce_sum x4 -> x0, other arithmetic: 16.2 us -> none  [attend_block(): running_sum = running_sum * decay_old + jnp.sum(weights, axis=-1)]
    le x4 -> x0, other arithmetic: 3.55 us -> none  [attend_block(): visible = key_pos[None, :] <= positions[:, None]]
    unnamed x5 -> x6, local copies, waits for them, and re-layouts: 6.63 us -> 4.92 us
  transfers between devices with their start and end apart: 3 -> 0, of which waited for: 3 -> 0; matrix products, arithmetic and copies ran while one was open for 1% -> 0% of each run, Pallas kernels for 0% -> 0%
where the time goes in v1:
time: 149 us; the launch traced here: 148 us
  Pallas kernels  142 us (95%)
  local copies, waits for them, and re-layouts  5.11 us (3%)
    pallas_call x1, Pallas kernels, fused_on_device(): pl.pallas_call(functools.partial(fused_kernel, n_ctx, n_blocks), out_shap...  142 us
    unnamed x6, local copies, waits for them, and re-layouts  4.92 us

profile of v1, /device:TPU:0, one launch (start us, length us, event | category | flops | bytes accessed | tf_op | source)
XLA Modules:
  0.0 148.4 jit_solution(12589721210286256157)
XLA Ops:
  0.0 0.0 copy-start
  0.0 0.0 copy-start.1
  0.0 2.6 %copy.12 = bf16[256,16,128]{2,0,1:T(8,128)(2,1)} copy(bf16[256,16,128]{2,1,0:T(8,128)(2,1)} %param.5) | data formatting | bytes 2097152 | tf_op args[0]
  2.6 0.0 copy-done
  2.6 0.0 copy-done.1
  2.6 0.2 copy_bitcast_fusion.1
  2.8 1.1 maximum_bitcast_fusion.kv_in
  3.9 142.2 %shard_map.55 = bf16[256,2304]{1,0:T(8,128)(2,1)} custom-call(bf16[16,256,128]{2,1,0:T(8,128)(2,1)} %bitcast.10, bf16[8,2,256,128]{3,2,1,0:T(8,128)(2,1)} %maximum_bitcast_fusion.kv_in, s32[1,256]{1,0:T(1,128)} %bitcast.11, bf16[2048,4608]{1,0:T(8,128)(2,1)} %w_hbm.1), custom_call_target="tpu_custom_call" | custom-call | tf_op jit(solution)/shard_map/pallas_call | solution.py:356
  146.0 2.4 %copy.14 = bf16[256,2304]{1,0:T(8,128)(2,1)} copy(bf16[256,2304]{1,0:T(8,128)(2,1)} %shard_map.55) | data formatting | bytes 2359296
Async XLA Ops:
  0.0 2.6 %copy-start = (bf16[256,8,128]{2,1,0:T(8,128)(2,1)S(1)}, bf16[256,8,128]{2,1,0:T(8,128)(2,1)}, u32[]{:S(2)}) copy-start(bf16[256,8,128]{2,1,0:T(8,128)(2,1)} %param.7) | copy-start | bytes 1572868
  0.0 2.6 %copy-start.1 = (bf16[256,8,128]{2,1,0:T(8,128)(2,1)S(1)}, bf16[256,8,128]{2,1,0:T(8,128)(2,1)}, u32[]{:S(2)}) copy-start(bf16[256,8,128]{2,1,0:T(8,128)(2,1)} %param.6) | copy-start | bytes 1572868

commit v2 on v1

--- a/solution.py
+++ b/solution.py
@@ -72,7 +72,7 @@
 
 def fused_kernel(
     n_ctx, n_blocks, q_in, kv_in, pos_in, w_hbm, out_ref,
-    kvbuf, qbuf, posbuf, qcol, m_ref, acc_ref, obuf, attbuf, w_vmem, sendbuf, recvbuf, ownbuf,
+    kvbuf, qbuf, posbuf, qcol, m_ref, acc_ref, obuf, attbuf, w_vmem, sendbuf, recvbuf, ownbuf, key_t,
     w_sem, pos_send, pos_recv, kvq_send, kvq_recv, q_send, q_recv,
     up_send, down_send, below_recv, above_recv, att_send, att_recv, y_send, y_recv,
 ):
@@ -196,31 +196,42 @@
         key_pos = jnp.concatenate([posbuf[layer * QUAD + i] for i in range(QUAD)], axis=1)
         key_pos = key_pos.astype(jnp.float32)
 
+        key_row = key_pos
+        key_t[...] = kvbuf[layer, g, 0].T
+        lanes = key_row.shape[1] // 128
+        q_rows = 256
+        tiles = tok_z // q_rows
+
+        def wide(a, count):
+            return jnp.concatenate([a] * count, axis=1)
+
         def tile(i, _):
-            r = i // QUAD
-            t = i % QUAD
-            q = qbuf[g * rep + r, rows(t), :]
-            keys = kvbuf[layer, g, 0]
+            span = pl.ds(pl.multiple_of(i * q_rows, q_rows), q_rows)
             values = kvbuf[layer, g, 1]
-            x = lax.dot_general(
-                q, keys, (((1,), (1,)), ((), ())), preferred_element_type=jnp.float32
-            ) * EXP2_SCALE
-            q_pos = qcol[rows(t), :][:, :1]
-            x = jnp.where(key_pos <= q_pos, x, NEG_BIG)
-            m_old = m_ref[g * rep + r, rows(t), :]
-            m_new = jnp.maximum(m_old, jnp.max(x, axis=1, keepdims=True))
-            m_ref[g * rep + r, rows(t), :] = m_new
-            decay = jnp.exp2(m_old - m_new)
-            weights = jnp.exp2(x - m_new[:, :1]).astype(jnp.bfloat16)
             extended = jnp.concatenate([values, jnp.ones_like(values)], axis=1)
-            new = jnp.dot(weights, extended, preferred_element_type=jnp.float32)
-            old = acc_ref[g * rep + r, rows(t), :]
-            acc_ref[g * rep + r, rows(t), :] = (
-                old * jnp.concatenate([decay, decay], axis=1) + new
-            )
+            heads = range(g * rep, (g + 1) * rep)
+            old_max = [m_ref[h, span, :] for h in heads]
+            old_acc = [acc_ref[h, span, :] for h in heads]
+            visible = key_row <= wide(qcol[span, :], lanes)
+            raw = [
+                jnp.dot(qbuf[h, span, :], key_t[...], preferred_element_type=jnp.float32)
+                for h in heads
+            ]
+            new_max, new_acc = [], []
+            for x, m_old, a_old in zip(raw, old_max, old_acc):
+                x = jnp.where(visible, x * EXP2_SCALE, NEG_BIG)
+                m_new = jnp.maximum(m_old, jnp.max(x, axis=1, keepdims=True))
+                decay = jnp.exp2(m_old - m_new)
+                weights = jnp.exp2(x - wide(m_new, lanes)).astype(jnp.bfloat16)
+                new = jnp.dot(weights, extended, preferred_element_type=jnp.float32)
+                new_max.append(m_new)
+                new_acc.append(a_old * wide(decay, 2) + new)
+            for h, m_new, a_new in zip(heads, new_max, new_acc):
+                m_ref[h, span, :] = m_new
+                acc_ref[h, span, :] = a_new
             return 0
 
-        lax.fori_loop(0, rep * QUAD, tile, 0)
+        lax.fori_loop(0, tiles, tile, 0, unroll=1)
 
     def att_copy(d, g):
         p = peer(d)
@@ -241,6 +252,36 @@
         cols = slice(g * rep * hd, (g + 1) * rep * hd)
         attbuf[s, :, cols] = obuf[rows(s), cols]
 
+    units = [(k, g, up) for k in range(1, nz) for g in range(groups) for up in (False, True)]
+    middle = (z > 0) & (z < nz - 1)
+
+    def exists(k, up):
+        return z - k >= 0 if up else z + k < nz
+
+    def arrive(i):
+        k, g, up = units[i]
+
+        @pl.when(exists(k, up))
+        def _():
+            if up:
+                wait_below(k, g)
+
+                @pl.when(z < nz - 1)
+                def _():
+                    up_chunk(k, g).start()
+            else:
+                wait_above(k, g)
+
+                @pl.when(z > 0)
+                def _():
+                    down_chunk(k, g).start()
+
+    def ahead(i):
+        if i < len(units):
+            @pl.when(middle)
+            def _():
+                arrive(i)
+
     for g in range(groups):
         own_parts(g)
         if g == 0:
@@ -251,34 +292,25 @@
                 for j in range(tok // 128):
                     piece = jnp.broadcast_to(line[:, j * 128:(j + 1) * 128], (128, 128))
                     qcol[i * tok + j * 128:i * tok + (j + 1) * 128, :] = piece.T
+        if g == groups - 1:
+            ahead(0)
         for d in (1, 2, 3):
             q_copy(d, g).wait_recv()
         compute(z, g)
 
-    for k in range(1, nz):
-        for g in range(groups):
-            @pl.when(z + k < nz)
-            def _():
-                wait_above(k, g)
-
-                @pl.when(z > 0)
-                def _():
-                    down_chunk(k, g).start()
-
-                compute(z + k, g)
-
-            @pl.when(z - k >= 0)
-            def _():
-                wait_below(k, g)
-
-                @pl.when(z < nz - 1)
-                def _():
-                    up_chunk(k, g).start()
-
-                compute(z - k, g)
-
-            if k == nz - 1:
-                finish(g)
+    for i, (k, g, up) in enumerate(units):
+        ahead(i + 1)
+
+        @pl.when(jnp.logical_not(middle))
+        def _():
+            arrive(i)
+
+        @pl.when(exists(k, up))
+        def _():
+            compute(z - k if up else z + k, g)
+
+        if k == nz - 1 and up:
+            finish(g)
     if nz == 1:
         for g in range(groups):
             finish(g)
@@ -371,6 +403,7 @@
             vmem((n_blocks, tok, width), jnp.bfloat16),
             vmem((n_blocks, tok, width), jnp.bfloat16),
             vmem((n_blocks, tok, width), jnp.float32),
+            vmem((hd, tok_z), jnp.bfloat16),
             dma((2,)),
             dma((n_ctx,)), dma((n_ctx,)),
             dma((QUAD, groups)), dma((QUAD, groups)),

time: 149 us -> 129 us (0.87)
  Pallas kernels: 142 us -> 123 us
    pallas_call x1, Pallas kernels: 142 us -> 123 us  [fused_on_device(): pl.pallas_call(functools.partial(fused_kernel, n_ctx, n_blocks), out_shap...]
where the time goes in v2:
time: 129 us
  Pallas kernels  123 us (95%)
  local copies, waits for them, and re-layouts  5.11 us (4%)
    pallas_call x1, Pallas kernels, fused_on_device(): pl.pallas_call(functools.partial(fused_kernel, n_ctx, n_blocks), out_shap...  123 us
    unnamed x6, local copies, waits for them, and re-layouts  4.92 us

profile of v2, /device:TPU:0, one launch (start us, length us, event | category | flops | bytes accessed | tf_op | source)
XLA Modules:
  0.0 129.1 jit_solution(11997016870095042806)
XLA Ops:
  0.0 0.0 copy-start
  0.0 0.0 copy-start.1
  0.0 2.6 %copy.12 = bf16[256,16,128]{2,0,1:T(8,128)(2,1)} copy(bf16[256,16,128]{2,1,0:T(8,128)(2,1)} %param.5) | data formatting | bytes 2097152 | tf_op args[0]
  2.6 0.0 copy-done
  2.6 0.0 copy-done.1
  2.6 0.2 copy_bitcast_fusion.1
  2.8 1.1 maximum_bitcast_fusion.kv_in
  3.9 122.8 %shard_map.55 = bf16[256,2304]{1,0:T(8,128)(2,1)} custom-call(bf16[16,256,128]{2,1,0:T(8,128)(2,1)} %bitcast.10, bf16[8,2,256,128]{3,2,1,0:T(8,128)(2,1)} %maximum_bitcast_fusion.kv_in, s32[1,256]{1,0:T(1,128)} %bitcast.11, bf16[2048,4608]{1,0:T(8,128)(2,1)} %w_hbm.1), custom_call_target="tpu_custom_call" | custom-call | tf_op jit(solution)/shard_map/pallas_call | solution.py:388
  126.7 2.4 %copy.14 = bf16[256,2304]{1,0:T(8,128)(2,1)} copy(bf16[256,2304]{1,0:T(8,128)(2,1)} %shard_map.55) | data formatting | bytes 2359296
Async XLA Ops:
  0.0 2.6 %copy-start = (bf16[256,8,128]{2,1,0:T(8,128)(2,1)S(1)}, bf16[256,8,128]{2,1,0:T(8,128)(2,1)}, u32[]{:S(2)}) copy-start(bf16[256,8,128]{2,1,0:T(8,128)(2,1)} %param.7) | copy-start | bytes 1572868
  0.0 2.6 %copy-start.1 = (bf16[256,8,128]{2,1,0:T(8,128)(2,1)S(1)}, bf16[256,8,128]{2,1,0:T(8,128)(2,1)}, u32[]{:S(2)}) copy-start(bf16[256,8,128]{2,1,0:T(8,128)(2,1)} %param.6) | copy-start | bytes 1572868
